TPU v7x, 256 devices: a whole 4x4x8 slice. The times are simulated.
256 devices in a mesh: vrow: 32 (over z, y), vcol: 8 (over x, core).
Axes of the slice: x: 4, y: 4, z: 8, core: 2. Of those that a mesh axis runs over, the one named last changes fastest.
Arguments:
- policy_hidden: bfloat16 [1024, 3584], P(None, 'vcol'), may hold values from -400 to 400
- ref_hidden: bfloat16 [1024, 3584], P(None, 'vcol'), may hold values from -400 to 400
- mix_num: int32 [1024], replicated, may hold values from 0 to 16, as said below
- mix_den: int32 [1024], replicated, may hold values from 2 to 16
- policy_unembed: bfloat16 [3584, 131072], P(None, ('vrow', 'vcol')), may hold values from -0.09375 to 0.09375
- ref_unembed: bfloat16 [3584, 131072], P(None, ('vrow', 'vcol')), may hold values from -0.09375 to 0.09375
Outputs:
- mix_logprobs: float32 [1024, 131072], P(None, ('vrow', 'vcol'))
Inputs may be any that keep to these rules, and one draw needn't show every extreme that they name: Each sequence's mix_num is at most its mix_den.
All inputs are finite; a program needn't handle non-finite values.
Results may differ from a plain program's by a relative error of at most 0.0003.
Values may be sent and summed in bfloat16 or wider, within the bound.
A program may use at most 64 MiB of HBM per device.

v0:
```python
import jax
import jax.numpy as jnp
from jax import lax
from jax.sharding import Mesh
from jax.sharding import PartitionSpec as P

VCOL = ("vcol_0", "vcol_1")
VROW_VCOL = ("vrow_0", "vrow_1", "vcol_0", "vcol_1")


def rows_first(arrays, axis, dims):
    turned = [jnp.moveaxis(a, dim, 0) for a, dim in zip(arrays, dims)]
    both = jnp.concatenate([t.reshape(len(t), -1) for t in turned], axis=1)
    filled, at, done = (lax.all_gather(both, axis, axis=0, tiled=True), 0, [])
    for t, dim in zip(turned, dims):
        slab = filled[:, at : at + t[0].size].reshape(-1, *t.shape[1:])
        done.append(jnp.moveaxis(slab, 0, dim))
        at += t[0].size
    return tuple(done)


def collected_together(value, axis):
    leaves = jax.tree.leaves(value)
    order = sorted(range(len(leaves)), key=lambda k: -leaves[k].size)
    width = (1, *leaves[order[0]].shape)[-1]
    lines = [
        jnp.pad(leaves[k].reshape(-1), (0, -leaves[k].size % width)).reshape(-1, width)
        for k in order
    ]
    both, at, found = (lax.all_gather(jnp.concatenate(lines), axis), 0, {})
    for k, line in zip(order, lines):
        slab = both[:, at : at + len(line)].reshape(len(both), -1)
        found[k] = slab[:, : leaves[k].size].reshape(-1, *leaves[k].shape)
        at += len(line)
    numbers = iter(range(len(leaves)))
    return jax.tree.map(lambda _: found[next(numbers)], value)


def joined_all(value, axes, combine):
    for axis in axes:
        pieces = collected_together(value, axis)
        value = jax.tree.map(lambda part: part[0], pieces)
        for k in range(1, lax.axis_size(axis)):
            value = combine(value, jax.tree.map(lambda part: part[k], pieces))
    return value


def combine_stats(first, second):
    high = jnp.maximum(first[0], second[0])
    total = first[1] * jnp.exp(first[0] - high) + second[1] * jnp.exp(second[0] - high)
    return (high, total)


def body(policy_hidden, ref_hidden, mix_num, mix_den, policy_unembed, ref_unembed):
    policy_full, ref_full = rows_first((policy_hidden, ref_hidden), VCOL, (1, 1))
    policy_logits = jnp.dot(policy_full, policy_unembed, preferred_element_type=jnp.float32)
    ref_logits = jnp.dot(ref_full, ref_unembed, preferred_element_type=jnp.float32)
    beta = (mix_num.astype(jnp.float32) / mix_den.astype(jnp.float32))[:, None]
    mixed = (1.0 - beta) * policy_logits + beta * ref_logits
    local_top = jnp.max(mixed, axis=1, keepdims=True)
    local_total = jnp.sum(jnp.exp(mixed - local_top), axis=1, keepdims=True)
    top, total = joined_all((local_top, local_total), VROW_VCOL, combine_stats)
    return mixed - top - jnp.log(total)


def solution(mesh):
    finer = Mesh(mesh.devices.reshape(8, 4, 4, 2), ("vrow_0", "vrow_1", "vcol_0", "vcol_1"))
    placed = (P(None, VCOL), P(None, VCOL), P(), P(), P(None, VROW_VCOL), P(None, VROW_VCOL))
    return jax.shard_map(
        body, mesh=finer, in_specs=placed, out_specs=P(None, VROW_VCOL), check_vma=False
    )
```

profile of v0, /device:TPU:1, one launch (start us, length us, event | category | flops | bytes accessed | tf_op | source)
XLA Modules:
  0.0 172.9 jit_solution(6092440054672598661)
XLA Ops:
  6.5 0.0 all-gather.6.cloned.1.call-start
  6.5 2.9 %pad_maximum_fusion = bf16[448,2048]{1,0:T(8,128)(2,1)} fusion(bf16[448,1024]{1,0:T(8,128)(2,1)} %bitcast.319, bf16[448,1024]{1,0:T(8,128)(2,1)} %bitcast.320), kind=kLoop, calls=%fused_computation.7 | loop fusion | flops 3670016 | bytes 3670016 | tf_op jit(solution)/shard_map/concatenate | solution.py:13
  9.4 0.0 all-gather.6.cloned.1.call-update
  9.5 0.0 copy-done
  9.5 0.0 copy-done.1
  9.5 82.9 %all-gather.6.cloned.1.call-done = bf16[3584,2048]{1,0:T(8,128)(2,1)} async-done(((bf16[448,2048]{1,0:T(8,128)(2,1)}), bf16[3584,2048]{1,0:T(8,128)(2,1)}) %all-gather.6.cloned.1.call-update) | async-done | bytes 14680080 | tf_op jit(solution)/shard_map/all_gather | solution.py:14
  92.4 7.5 %fusion = f32[1024,512]{0,1:T(8,128)S(1)} fusion(bf16[3584,512]{1,0:T(8,128)(2,1)} %param.11, bf16[3584,2048]{1,0:T(8,128)(2,1)} %all-gather.6.cloned.1.call-done), kind=kOutput, calls=%fused_computation | convolution fusion | flops 3758096384 | bytes 13107200 | tf_op jit(solution)/shard_map/dot_general | solution.py:57
  100.0 0.8 copy-done.2
  100.8 1.0 copy-done.3
  101.9 4.1 %fusion.62 = (f32[1024]{0:T(1024)S(1)}, f32[1024,512]{0,1:T(8,128)S(1)}) fusion(f32[1024,512]{0,1:T(8,128)S(1)} %fusion, f32[1024]{0:T(1024)S(1)} %get-tuple-element.14, bf16[3584,512]{1,0:T(8,128)(2,1)S(1)} %copy-done.3, bf16[3584,2048]{1,0:T(8,128)(2,1)S(1)} %copy-done.2, f32[1024]{0:T(1024)S(1)} %get-tuple-element.13), kind=kOutput, calls=%fused_computation.100 | convolution fusion | flops 3760192512 | bytes 15216640 | tf_op jit(solution)/shard_map/dot_general | solution.py:56
  106.0 0.3 exponential_reduce_fusion
  106.3 19.7 %all-gather = f32[16384,1]{0,1:T(1,128)S(1)} all-gather(f32[2048,1]{0,1:T(1,128)S(1)} %pad_maximum_fusion.1), channel_id=2, replica_groups=mesh['vrow_0'=8,'vrow_1'=4,'vcol_0'=4,'vcol_1'=2] {'vrow_0'}, dimensions={0}, use_global_device_ids=true | all-gather | bytes 73728 | tf_op jit(solution)/shard_map/all_gather | solution.py:30
  126.1 0.1 fusion.25
  126.2 9.5 %all-gather.1 = f32[8192,1]{0,1:T(1,128)S(1)} all-gather(f32[2048,1]{0,1:T(1,128)S(1)} %pad_maximum_fusion.2), channel_id=3, replica_groups=mesh['vrow_0'=8,'vrow_1'=4,'vcol_0'=4,'vcol_1'=2] {'vrow_1'}, dimensions={0}, use_global_device_ids=true | all-gather | bytes 40960 | tf_op jit(solution)/shard_map/all_gather | solution.py:30
  135.7 0.5 broadcast.16
  136.2 0.7 reduce.12
  137.0 0.1 fusion.16
  137.1 9.0 %all-gather.2 = f32[8192,1]{0,1:T(1,128)S(1)} all-gather(f32[2048,1]{0,1:T(1,128)S(1)} %pad_maximum_fusion.3), channel_id=4, replica_groups=mesh['vrow_0'=8,'vrow_1'=4,'vcol_0'=4,'vcol_1'=2] {'vcol_0'}, dimensions={0}, use_global_device_ids=true | all-gather | bytes 40960 | tf_op jit(solution)/shard_map/all_gather | solution.py:30
  146.1 0.7 reduce.13
  146.9 0.1 fusion.7
  146.9 13.7 %all-gather.3 = f32[4096,1]{0,1:T(1,128)S(1)} all-gather(f32[2048,1]{0,1:T(1,128)S(1)} %pad_maximum_fusion.4), channel_id=5, replica_groups=mesh['vrow_0'=8,'vrow_1'=4,'vcol_0'=4,'vcol_1'=2] {'vcol_1'}, dimensions={0}, use_global_device_ids=true | all-gather | bytes 24576 | tf_op jit(solution)/shard_map/all_gather | solution.py:30
  160.6 0.7 reduce.14
  161.4 1.8 %subtract_subtract_fusion = f32[1024,512]{0,1:T(8,128)} fusion(f32[1024,512]{0,1:T(8,128)S(1)} %get-tuple-element.20, f32[1024]{0:T(1024)S(1)} %get-tuple-element.5, f32[1024]{0:T(1024)S(1)} %get-tuple-element.6), kind=kLoop, calls=%fused_computation.4 | loop fusion | flops 1048576 | bytes 4202496 | tf_op jit(solution)/shard_map/sub | solution.py:63
  163.1 2.9 %copy.8 = f32[1024,512]{1,0:T(8,128)} copy(f32[1024,512]{0,1:T(8,128)} %subtract_subtract_fusion) | data formatting | bytes 4194304 | tf_op jit(solution)/shard_map/sub | solution.py:63
  (15 shorter events, 0.2 us)
Async XLA Ops:
  6.5 85.9 %all-gather.6.cloned.1.call-start = ((), (), s32[]{:S(2)}) async-start(), calls=%async_computation | async-start | bytes 16515072 | tf_op jit(solution)/shard_map/all_gather | solution.py:14
  6.5 2.9 %copy-start = (s32[1024]{0:T(1024)S(1)}, s32[1024]{0:T(1024)}, u32[]{:S(2)}) copy-start(s32[1024]{0:T(1024)} %param.9) | copy-start | bytes 12292
  6.5 2.9 %copy-start.1 = (s32[1024]{0:T(1024)S(1)}, s32[1024]{0:T(1024)}, u32[]{:S(2)}) copy-start(s32[1024]{0:T(1024)} %param.8) | copy-start | bytes 12292
  92.4 8.4 %copy-start.2 = (bf16[3584,2048]{1,0:T(8,128)(2,1)S(1)}, bf16[3584,2048]{1,0:T(8,128)(2,1)}, u32[]{:S(2)}) copy-start(bf16[3584,2048]{1,0:T(8,128)(2,1)} %all-gather.6.cloned.1.call-done) | copy-start | bytes 44040196
  92.4 9.4 %copy-start.3 = (bf16[3584,512]{1,0:T(8,128)(2,1)S(1)}, bf16[3584,512]{1,0:T(8,128)(2,1)}, u32[]{:S(2)}) copy-start(bf16[3584,512]{1,0:T(8,128)(2,1)} %param.10) | copy-start | bytes 11010052
Sparse Core Ops, SparseCore 0:
  9.6 82.7 all-gather.5
where the time goes:
time: 173 us
  waiting for transfers between devices  82.9 us (48%)
  blocking collectives  52 us (30%)
  between operations  13.5 us (8%)
  matrix products  11.7 us (7%)
  other arithmetic  7.39 us (4%)
  local copies, waits for them, and re-layouts  5.37 us (3%)
    all_gather x1, waiting for transfers between devices, rows_first(): filled, at, done = (lax.all_gather(both, axis, axis=0, tiled=True), 0, [])  82.9 us
    all_gather x4, blocking collectives, collected_together(): both, at, found = (lax.all_gather(jnp.concatenate(lines), axis), 0, {})  52 us
    dot_general x1, matrix products, body(): jnp.dot(ref_full, ref_unembed, preferred_element_type=jnp.float32)  7.54 us
    dot_general x1, matrix products, body(): jnp.dot(policy_full, policy_unembed, preferred_element_type=jnp.float32)  4.12 us
  transfers between devices with their start and end apart: 1, of which 1 were waited for; matrix products, arithmetic and copies ran while one was open for 0% of the time, Pallas kernels for 0%

commit v1 on v0

v1 whole, which is shorter than its diff:
```python
import functools

import jax
import jax.numpy as jnp
from jax import lax
from jax.experimental import pallas as pl
from jax.experimental.pallas import tpu as pltpu
from jax.sharding import Mesh
from jax.sharding import PartitionSpec as P

MESH = pl.DeviceIdType.MESH
VCOL = ("vcol_0", "vcol_1")
VROW_VCOL = ("vrow_0", "vrow_1", "vcol_0", "vcol_1")

HALF = 512
QUARTER = 128
CHUNK = 32
PIECES = QUARTER // CHUNK
FEATS = 448
FULL = 384
WIRE = 2 * FEATS
LAG = 3

XP, XM, YP, YM, ZP, ZM = range(6)


def place(flow, r):
    if flow in (XP, YP, YM):
        early, mid = 2, 6
    else:
        early, mid = 4, 7
    if r < 2 * PIECES:
        slot, piece = early + r % 2, r // 2
    elif r < 3 * PIECES:
        slot, piece = mid, r - 2 * PIECES
    else:
        slot, piece = {XP: 2, XM: 5, YP: 3, YM: 6, ZP: 4, ZM: 7}[flow], r - 3 * PIECES
    if r >= 3 * PIECES:
        return slot, 2, piece
    return slot, {XP: 0, XM: 0, YP: 1, YM: 3, ZP: 1, ZM: 3}[flow], piece


def kernel(
    ph, rh, num, den, pw, rw, mixed, lse,
    buf, other, raw, wb, acc, beta, stat, xyin, stat2, zin, part, partin,
    hid_sem, w_sem, wr_sem, ws_sem, recv_sem, send_sem, peer_sem, out_sem, xy_sem, z_sem, l_sem,
):
    z, y = lax.axis_index("vrow_0"), lax.axis_index("vrow_1")
    x, c = lax.axis_index("vcol_0"), lax.axis_index("vcol_1")
    o = 1 - c
    colour = (y + z) % 4
    xs = [x, (x + 1) % 4, (x + 3) % 4, (x + 2) % 4]
    target = {
        XP: (z, y, (x + 3) % 4, c),
        XM: (z, y, (x + 1) % 4, c),
        YP: (z, (y + 3) % 4, x, c),
        YM: (z, (y + 1) % 4, x, c),
        ZP: ((z + 7) % 8, y, x, c),
        ZM: ((z + 1) % 8, y, x, c),
    }
    peer = (z, y, x, o)

    def remote(src, dst, send, recv, device):
        return pltpu.make_async_remote_copy(
            src_ref=src, dst_ref=dst, send_sem=send, recv_sem=recv, device_id=device, device_id_type=MESH
        )

    mine = pl.ds(pl.multiple_of(c * HALF, HALF), HALF)
    theirs = pl.ds(pl.multiple_of(o * HALF, HALF), HALF)
    hidden = [
        pltpu.make_async_copy(ph, raw.at[0], hid_sem.at[0]),
        pltpu.make_async_copy(rh, raw.at[1], hid_sem.at[1]),
        pltpu.make_async_copy(ph.at[mine, pl.ds(0, FULL)], buf.at[0, :, pl.ds(0, FULL)], hid_sem.at[2]),
        pltpu.make_async_copy(rh.at[mine, pl.ds(0, FULL)], buf.at[0, :, pl.ds(512, FULL)], hid_sem.at[3]),
        pltpu.make_async_copy(ph.at[theirs, pl.ds(0, FULL)], other.at[:, pl.ds(0, FULL)], hid_sem.at[4]),
        pltpu.make_async_copy(rh.at[theirs, pl.ds(0, FULL)], other.at[:, pl.ds(512, FULL)], hid_sem.at[5]),
    ]
    for copy in hidden:
        copy.start()

    barrier = pltpu.get_barrier_semaphore()
    near = [target[f] for f in range(6)]
    near += [(z, y, (x + 3) % 4, o), (z, y, (x + 1) % 4, o), peer]
    for device in near:
        pl.semaphore_signal(barrier, inc=1, device_id=device, device_id_type=MESH)

    def weight_parts(base, dst):
        base = pl.multiple_of(base * FEATS, 64)
        return [
            (pw.at[pl.ds(base, FEATS)], dst.at[pl.ds(0, FEATS)]),
            (rw.at[pl.ds(base + FULL, 64)], dst.at[pl.ds(576, 64)]),
            (rw.at[pl.ds(base, FULL)], dst.at[pl.ds(640, FULL)]),
        ]

    for slot in range(8):
        base = xs[slot // 2] * 2 + (c if slot % 2 == 0 else o)
        for src, dst in weight_parts(base, wb.at[0, slot]):
            pltpu.make_async_copy(src, dst, w_sem.at[slot]).start()

    for k in range(4):
        row = pl.ds(c * 4 + k, 1)
        value = num[row, :].astype(jnp.float32) / den[row, :].astype(jnp.float32)
        beta[pl.ds(k * QUARTER, QUARTER), :] = jnp.broadcast_to(value, (QUARTER, 128)).T
    for h in range(2):
        for slot in range(8):
            wb[h, slot, pl.ds(FEATS, 128), :] = jnp.zeros((128, HALF), jnp.bfloat16)

    for copy in hidden:
        copy.wait()
    buf[0, :, pl.ds(FULL, 128)] = jnp.concatenate(
        [raw[0, mine, pl.ds(FULL, 64)], raw[1, mine, pl.ds(FULL, 64)]], axis=1
    )
    other[:, pl.ds(FULL, 128)] = jnp.concatenate(
        [raw[0, theirs, pl.ds(FULL, 64)], raw[1, theirs, pl.ds(FULL, 64)]], axis=1
    )
    pl.semaphore_wait(barrier, len(near))

    def rows(offset, piece):
        quarter = (colour + offset) % 4
        return pl.ds(pl.multiple_of(quarter * QUARTER + piece * CHUNK, CHUNK), CHUNK)

    def send(flow, r, src, cross=False):
        slot, _, _ = place(flow, r)
        source, window = src
        device = target[flow]
        if cross:
            device = (*device[:3], o)
        remote(source.at[window], buf.at[slot, window], send_sem.at[flow], recv_sem.at[flow, r], device).start()

    def arrived(flow, r):
        slot, offset, piece = place(flow, r)
        ref = buf.at[slot, rows(offset, piece)]
        remote(ref, ref, send_sem.at[flow], recv_sem.at[flow, r], target[flow]).wait_recv()
        return buf.at[slot], rows(offset, piece)

    for k in range(PIECES):
        for flow in (XP, XM):
            send(flow, 2 * k, (buf.at[0], rows(0, k)))
            send(flow, 2 * k + 1, (other, rows(0, k)), cross=True)
    swap = remote(other, buf.at[1], peer_sem.at[0], peer_sem.at[1], peer)
    swap.start()
    for slot in range(8):
        base = xs[slot // 2] * 2 + (o if slot % 2 == 0 else c)
        for src, dst in weight_parts(base, wb.at[1, slot]):
            remote(src, dst, ws_sem, wr_sem.at[slot], peer).start()

    seen = set()

    def weights(slot):
        if slot in seen:
            return
        seen.add(slot)
        own, got = wb.at[0, slot, pl.ds(0, WIRE)], wb.at[1, slot, pl.ds(0, WIRE)]
        pltpu.make_async_copy(own, own, w_sem.at[slot]).wait()
        remote(got, got, ws_sem, wr_sem.at[slot], peer).wait_recv()

    def block(offset):
        quarter = (colour + offset) % 4
        return pl.ds(pl.multiple_of(quarter * QUARTER, QUARTER), QUARTER)

    def multiply(slot, offsets, first=False):
        weights(slot)
        parts = [buf[slot, block(i), :] for i in offsets]
        left = parts[0] if len(parts) == 1 else jnp.concatenate(parts, axis=0)
        for h in range(2):
            policy = jnp.dot(left[:, :512], wb[h, slot, pl.ds(0, 512), :], preferred_element_type=jnp.float32)
            ref = jnp.dot(left[:, 384:], wb[h, slot, pl.ds(512, 512), :], preferred_element_type=jnp.float32)
            for n, i in enumerate(offsets):
                b = jnp.concatenate([beta[block(i), :]] * 4, axis=1)
                at = slice(n * QUARTER, (n + 1) * QUARTER)
                value = (1.0 - b) * policy[at] + b * ref[at]
                acc[h, block(i), :] = value if first else acc[h, block(i), :] + value

    def out_rows(offset):
        quarter = (colour + offset) % 4
        return pl.ds(pl.multiple_of(c * HALF + quarter * QUARTER, QUARTER), QUARTER)

    def out_copies(offset):
        near = pltpu.make_async_copy(acc.at[0, block(offset)], mixed.at[out_rows(offset)], out_sem.at[0, offset])
        far = remote(
            acc.at[1, block(offset)], mixed.at[out_rows(offset)], out_sem.at[1, offset], out_sem.at[2, offset], peer
        )
        return near, far

    def finish(offset):
        tiles = [acc[h, block(offset), pl.ds(j * 128, 128)] for h in range(2) for j in range(4)]
        high = functools.reduce(jnp.maximum, tiles)
        total = functools.reduce(jnp.add, [jnp.exp(t - high) for t in tiles])
        high, total = high.T, total.T
        top = jnp.max(high, axis=0, keepdims=True)
        summed = jnp.sum(total * jnp.exp(high - top), axis=0, keepdims=True)
        quarter = (colour + offset) % 4
        stat[pl.ds(quarter, 1), :] = top
        stat[pl.ds(quarter + 4, 1), :] = summed
        for copy in out_copies(offset):
            copy.start()

    def spread(r):
        plus, minus = arrived(XP, r), arrived(XM, r)
        if r < 3 * PIECES:
            for flow in (YP, YM):
                send(flow, r, plus)
            for flow in (ZP, ZM):
                send(flow, r, minus)
        if r < 2 * PIECES:
            if r % 2 == 0:
                send(XP, 2 * PIECES + r // 2, plus)
            else:
                send(XM, 2 * PIECES + r // 2, minus)
        if 2 * PIECES <= r < 3 * PIECES:
            k = r - 2 * PIECES
            send(XP, 3 * PIECES + k, (buf.at[0], rows(2, k)))
            send(XM, 3 * PIECES + k, (other, rows(2, k)), cross=True)

    def relay(r):
        got = {flow: arrived(flow, r) for flow in (YP, YM, ZP, ZM)}
        if r < 2 * PIECES:
            if r % 2 == 1:
                send(YP, 3 * PIECES + r // 2, got[YP])
            else:
                send(ZP, 3 * PIECES + r // 2, got[ZP])
        elif r < 3 * PIECES:
            send(YM, PIECES + r, got[YM])
            send(ZM, PIECES + r, got[ZM])

    tasks = {
        0: [lambda: multiply(0, (0, 1, 2, 3), first=True)],
        3: [lambda: (swap.wait_recv(), multiply(1, (0, 1, 2, 3)))],
        7: [lambda: multiply(2, (0,)), lambda: multiply(3, (0,))],
        8: [lambda: multiply(4, (0,)), lambda: multiply(5, (0,))],
        10: [lambda: multiply(2, (1, 3))],
        11: [lambda: multiply(3, (1, 3)), lambda: multiply(4, (1, 3))],
        12: [lambda: multiply(5, (1, 3)), lambda: multiply(6, (0,))],
        13: [lambda: multiply(7, (0,))],
        14: [lambda: multiply(6, (1, 3)), lambda: finish(0)],
        15: [lambda: multiply(7, (1, 3)), lambda: multiply(2, (2,))],
        16: [lambda: multiply(5, (2,)), lambda: finish(1)],
        17: [lambda: finish(3)],
        18: [lambda: multiply(s, (2,)) for s in (3, 4, 6, 7)] + [lambda: finish(2)],
    }
    tasks[18] = [functools.partial(multiply, s, (2,)) for s in (3, 4, 6, 7)] + [lambda: finish(2)]
    for r in range(4 * PIECES + LAG):
        if r < 4 * PIECES:
            spread(r)
        if r >= LAG:
            relay(r - LAG)
        for task in tasks.get(r, ()):
            task()

    def combine(pairs):
        top = functools.reduce(jnp.maximum, [p[0] for p in pairs])
        return top, functools.reduce(jnp.add, [p[1] * jnp.exp(p[0] - top) for p in pairs])

    def halves(ref):
        return ref[pl.ds(0, 4), :], ref[pl.ds(4, 4), :]

    sends = []
    for k in range(1, 16):
        device = (z, (y + k // 4) % 4, (x + k % 4) % 4, c)
        sends.append(remote(stat, xyin.at[k], xy_sem.at[0, k], xy_sem.at[1, k], device))
        sends[-1].start()
    for copy in sends:
        copy.wait_recv()
    top, total = combine([halves(stat)] + [halves(xyin.at[k]) for k in range(1, 16)])
    stat2[pl.ds(0, 4), :] = top
    stat2[pl.ds(4, 4), :] = total
    for k in range(1, 8):
        copy = remote(stat2, zin.at[k], z_sem.at[0, k], z_sem.at[1, k], ((z + k) % 8, y, x, c))
        copy.start()
        sends.append(copy)
    for copy in sends[15:]:
        copy.wait_recv()
    top, total = combine([(top, total)] + [halves(zin.at[k]) for k in range(1, 8)])
    value = top + jnp.log(total)
    part[pl.ds(0, 4), :] = value
    part[pl.ds(4, 4), :] = value
    last = remote(part, partin, l_sem.at[0], l_sem.at[1], peer)
    last.start()
    lse[c] = part[...]

    for copy in sends:
        copy.wait_send()
    for flow in range(6):
        remote(buf.at[0], buf.at[0], send_sem.at[flow], recv_sem.at[flow, 0], peer).wait_send()
    gone = wb.at[0, :, pl.ds(0, WIRE)]
    remote(gone, gone, ws_sem, wr_sem.at[0], peer).wait_send()
    swap.wait_send()
    for offset in range(4):
        near, far = out_copies(offset)
        near.wait()
        far.wait()
    last.wait()
    lse[o] = partin[...]


def body(policy_hidden, ref_hidden, mix_num, mix_den, policy_unembed, ref_unembed):
    hbm = pl.BlockSpec(memory_space=pl.ANY)
    vmem = pl.BlockSpec(memory_space=pltpu.VMEM)
    dma = pltpu.SemaphoreType.DMA
    mixed, lse = pl.pallas_call(
        kernel,
        out_shape=(
            jax.ShapeDtypeStruct((2 * HALF, HALF), jnp.float32),
            jax.ShapeDtypeStruct((2, 8, 128), jnp.float32),
        ),
        in_specs=[hbm, hbm, vmem, vmem, hbm, hbm],
        out_specs=(hbm, vmem),
        scratch_shapes=[
            pltpu.VMEM((8, HALF, WIRE), jnp.bfloat16),
            pltpu.VMEM((HALF, WIRE), jnp.bfloat16),
            pltpu.VMEM((2, 2 * HALF, FEATS), jnp.bfloat16),
            pltpu.VMEM((2, 8, 1024, HALF), jnp.bfloat16),
            pltpu.VMEM((2, HALF, HALF), jnp.float32),
            pltpu.VMEM((HALF, 128), jnp.float32),
            pltpu.VMEM((8, 128), jnp.float32),
            pltpu.VMEM((16, 8, 128), jnp.float32),
            pltpu.VMEM((8, 128), jnp.float32),
            pltpu.VMEM((8, 8, 128), jnp.float32),
            pltpu.VMEM((8, 128), jnp.float32),
            pltpu.VMEM((8, 128), jnp.float32),
            dma((6,)),
            dma((8,)),
            dma((8,)),
            dma(()),
            dma((6, 4 * PIECES)),
            dma((6,)),
            dma((2,)),
            dma((3, 4)),
            dma((2, 16)),
            dma((2, 8)),
            dma((2,)),
        ],
        compiler_params=pltpu.CompilerParams(collective_id=0, has_side_effects=True),
        name="mixture",
    )(
        policy_hidden,
        ref_hidden,
        mix_num.reshape(8, 128),
        mix_den.reshape(8, 128),
        policy_unembed,
        ref_unembed,
    )
    return mixed - lse[:, :4].reshape(2 * HALF, 1)


def solution(mesh):
    finer = Mesh(mesh.devices.reshape(8, 4, 4, 2), VROW_VCOL)
    placed = (P(None, VCOL), P(None, VCOL), P(), P(), P(None, VROW_VCOL), P(None, VROW_VCOL))
    return jax.shard_map(
        body, mesh=finer, in_specs=placed, out_specs=P(None, VROW_VCOL), check_vma=False
    )
```

time: 173 us -> 62.9 us (0.36)
  waiting for transfers between devices: 82.9 us -> 0 us
  Pallas kernels: 0 us -> 55.3 us
  blocking collectives: 52 us -> 0 us
  between operations: 13.5 us -> 0.01 us
  matrix products: 11.7 us -> 0 us
  other arithmetic: 7.39 us -> 3.11 us
    all_gather x1 -> x0, waiting for transfers between devices: 82.9 us -> none  [rows_first(): filled, at, done = (lax.all_gather(both, axis, axis=0, tiled=True), 0, [])]
    pallas_call x0 -> x1, Pallas kernels: none -> 55.3 us  [body(): pl.pallas_call(kernel, out_shape=(jax.ShapeDtypeStruct((2 * HALF, HALF),...]
    all_gather x4 -> x0, blocking collectives: 52 us -> none  [collected_together(): both, at, found = (lax.all_gather(jnp.concatenate(lines), axis), 0, {})]
    dot_general x2 -> x0, matrix products: 11.7 us -> none  [the longest x1 7.54 us: body(): jnp.dot(ref_full, ref_unembed, preferred_element_type=jnp.float32)]
    concatenate x5 -> x0, other arithmetic: 2.93 us -> none  [the longest x1 2.89 us: rows_first(): both = jnp.concatenate([t.reshape(len(t), -1) for t in turned], axis=1)]
    sub x1 -> x0, local copies, waits for them, and re-layouts: 2.88 us -> none  [body(): return mixed - top - jnp.log(total)]
    all_gather x3 -> x0, other arithmetic: 2.12 us -> none  [collected_together(): both, at, found = (lax.all_gather(jnp.concatenate(lines), axis), 0, {})]
    unnamed x9 -> x4, local copies, waits for them, and re-layouts: 1.92 us -> 3.63 us
  transfers between devices with their start and end apart: 1 -> 0, of which waited for: 1 -> 0; matrix products, arithmetic and copies ran while one was open for 0% -> 0% of each run, Pallas kernels for 0% -> 0%
where the time goes in v1:
time: 62.9 us; the launch traced here: 62.7 us
  Pallas kernels  55.3 us (88%)
  local copies, waits for them, and re-layouts  4.33 us (7%)
  other arithmetic  3.11 us (5%)
    pallas_call x1, Pallas kernels, body(): pl.pallas_call(kernel, out_shape=(jax.ShapeDtypeStruct((2 * HALF, HALF),...  55.3 us
    unnamed x4, local copies, waits for them, and re-layouts  3.63 us
    sub x1, other arithmetic, body(): return mixed - lse[:, :4].reshape(2 * HALF, 1)  3.11 us

profile of v1, /device:TPU:1, one launch (start us, length us, event | category | flops | bytes accessed | tf_op | source)
XLA Modules:
  0.0 62.7 jit_solution(1869537379388104161)
XLA Ops:
  0.0 0.0 copy-start
  0.0 2.3 %copy.7.ph = bf16[1024,448]{1,0:T(8,128)(2,1)} copy(bf16[1024,448]{0,1:T(8,128)(2,1)} %param.6) | data formatting | bytes 1835008 | tf_op args[0]
  2.3 0.0 copy-done
  2.3 1.3 %copy.8.rh = bf16[1024,448]{1,0:T(8,128)(2,1)} copy(bf16[1024,448]{0,1:T(8,128)(2,1)S(1)} %copy-done) | data formatting | bytes 1835008 | tf_op args[1]
  3.6 55.3 %mixture.1 = (f32[1024,512]{1,0:T(8,128)}, f32[2,8,128]{2,1,0:T(8,128)}) custom-call(bf16[1024,448]{1,0:T(8,128)(2,1)} %copy.7.ph, bf16[1024,448]{1,0:T(8,128)(2,1)} %copy.8.rh, s32[8,128]{1,0:T(8,128)} %bitcast.4, s32[8,128]{1,0:T(8,128)} %bitcast.5, bf16[3584,512]{1,0:T(8,128)(2,1)} %pw.1, bf16[3584,512]{1,0:T(8,128)(2,1)} %rw.1), custom_call_target="tpu_custom_call" | custom-call | tf_op jit(solution)/shard_map/mixture/pallas_call | solution.py:300
  58.9 0.7 %slice.3 = f32[2,4,128]{2,1,0:T(4,128)S(1)} slice(f32[2,8,128]{2,1,0:T(8,128)} %get-tuple-element.8), slice={[0:2], [0:4], [0:128]} | slice | bytes 8192 | tf_op jit(solution)/shard_map/slice | solution.py:343
  59.6 3.1 %broadcast_subtract_fusion = f32[1024,512]{1,0:T(8,128)} fusion(f32[1024,512]{1,0:T(8,128)} %get-tuple-element.7, f32[1024]{0:T(1024)S(1)} %bitcast.3), kind=kLoop, calls=%fused_computation | loop fusion | flops 524288 | bytes 4198400 | tf_op jit(solution)/shard_map/sub | solution.py:343
Async XLA Ops:
  0.0 2.3 %copy-start = (bf16[1024,448]{0,1:T(8,128)(2,1)S(1)}, bf16[1024,448]{0,1:T(8,128)(2,1)}, u32[]{:S(2)}) copy-start(bf16[1024,448]{0,1:T(8,128)(2,1)} %param.7) | copy-start | bytes 2752516

commit v2 on v1

v2 whole, which is shorter than its diff:
```python
import functools

import jax
import jax.numpy as jnp
from jax import lax
from jax.experimental import pallas as pl
from jax.experimental.pallas import tpu as pltpu
from jax.sharding import Mesh
from jax.sharding import PartitionSpec as P

MESH = pl.DeviceIdType.MESH
VCOL = ("vcol_0", "vcol_1")
VROW_VCOL = ("vrow_0", "vrow_1", "vcol_0", "vcol_1")

HALF = 512
QUARTER = 128
CHUNK = 32
PIECES = QUARTER // CHUNK
FEATS = 448
FULL = 384
WIRE = 2 * FEATS
GROUP = (0, 1, 2, 2, 3, 3, 4, 4)
LAG = 3

XP, XM, YP, YM, ZP, ZM = range(6)


def place(flow, r):
    if flow in (XP, YP, YM):
        early, mid = 2, 6
    else:
        early, mid = 4, 7
    if r < 2 * PIECES:
        slot, piece = early + r % 2, r // 2
    elif r < 3 * PIECES:
        slot, piece = mid, r - 2 * PIECES
    else:
        slot, piece = {XP: 2, XM: 5, YP: 3, YM: 6, ZP: 4, ZM: 7}[flow], r - 3 * PIECES
    if r >= 3 * PIECES:
        return slot, 2, piece
    return slot, {XP: 0, XM: 0, YP: 1, YM: 3, ZP: 1, ZM: 3}[flow], piece


def kernel(
    ph, rh, num, den, pw, rw, out,
    buf, other, raw, wb, acc, theirs, ratio, beta, stat, xyin, stat2, zin,
    hid_sem, w_sem, wr_sem, ws_sem, recv_sem, send_sem, peer_sem, far_sem, xy_sem, z_sem,
):
    z, y = lax.axis_index("vrow_0"), lax.axis_index("vrow_1")
    x, c = lax.axis_index("vcol_0"), lax.axis_index("vcol_1")
    o = 1 - c
    colour = (y + z) % 4
    xs = [x, (x + 1) % 4, (x + 3) % 4, (x + 2) % 4]
    target = {
        XP: (z, y, (x + 3) % 4, c),
        XM: (z, y, (x + 1) % 4, c),
        YP: (z, (y + 3) % 4, x, c),
        YM: (z, (y + 1) % 4, x, c),
        ZP: ((z + 7) % 8, y, x, c),
        ZM: ((z + 1) % 8, y, x, c),
    }
    peer = (z, y, x, o)

    def remote(src, dst, send, recv, device):
        return pltpu.make_async_remote_copy(
            src_ref=src, dst_ref=dst, send_sem=send, recv_sem=recv, device_id=device, device_id_type=MESH
        )

    def lanes(core, offset):
        return pl.ds(pl.multiple_of((core * 4 + (colour + offset) % 4) * QUARTER, QUARTER), QUARTER)

    for i in range(4):
        for n, core in enumerate((c, o)):
            at = lanes(core, i)
            pltpu.make_async_copy(ph.at[:, at], raw.at[0, :, at], hid_sem.at[min(i, 1)]).start()
            pltpu.make_async_copy(rh.at[:, at], raw.at[1, :, at], hid_sem.at[min(i, 1)]).start()

    pltpu.make_async_copy(num, ratio.at[0], hid_sem.at[2]).start()
    pltpu.make_async_copy(den, ratio.at[1], hid_sem.at[2]).start()

    barrier = pltpu.get_barrier_semaphore()
    near = [target[f] for f in range(6)]
    near += [(z, y, (x + 3) % 4, o), (z, y, (x + 1) % 4, o), peer]
    for device in near:
        pl.semaphore_signal(barrier, inc=1, device_id=device, device_id_type=MESH)

    def weight_parts(base, dst):
        base = pl.multiple_of(base * FEATS, 64)
        return [
            (pw.at[pl.ds(base, FEATS)], dst.at[pl.ds(0, FEATS)]),
            (rw.at[pl.ds(base + FULL, 64)], dst.at[pl.ds(576, 64)]),
            (rw.at[pl.ds(base, FULL)], dst.at[pl.ds(640, FULL)]),
        ]

    def block(offset):
        quarter = (colour + offset) % 4
        return pl.ds(pl.multiple_of(quarter * QUARTER, QUARTER), QUARTER)

    def loaded(k, blocks):
        here = raw.at[:, :, pl.ds(0, blocks * QUARTER)]
        pltpu.make_async_copy(here, here, hid_sem.at[k]).wait()

    def pack(i):
        for n, core in enumerate((c, o)):
            at = lanes(core, i)
            turned = jnp.concatenate(
                [raw[0, :, at], raw[1, pl.ds(FULL, 64), at], raw[1, pl.ds(0, FULL), at]], axis=0
            ).T
            if n == 0:
                buf[0, block(i), :] = turned
            else:
                other[block(i), :] = turned

    loaded(0, 2)
    pack(0)
    pl.semaphore_wait(barrier, len(near))

    def rows(offset, piece):
        quarter = (colour + offset) % 4
        return pl.ds(pl.multiple_of(quarter * QUARTER + piece * CHUNK, CHUNK), CHUNK)

    def send(flow, r, src, cross=False):
        slot, _, _ = place(flow, r)
        source, window = src
        device = target[flow]
        if cross:
            device = (*device[:3], o)
        remote(source.at[window], buf.at[slot, window], send_sem.at[flow], recv_sem.at[flow, r], device).start()

    def arrived(flow, r):
        slot, offset, piece = place(flow, r)
        ref = buf.at[slot, rows(offset, piece)]
        remote(ref, ref, send_sem.at[flow], recv_sem.at[flow, r], target[flow]).wait_recv()
        return buf.at[slot], rows(offset, piece)

    for k in range(PIECES):
        for flow in (XP, XM):
            send(flow, 2 * k, (buf.at[0], rows(0, k)))
            send(flow, 2 * k + 1, (other, rows(0, k)), cross=True)
    def fetch(slots):
        for slot in slots:
            base = xs[slot // 2] * 2 + (o if slot % 2 == 0 else c)
            for src, dst in weight_parts(base, wb.at[1, slot]):
                remote(src, dst, ws_sem, wr_sem.at[GROUP[slot]], peer).start()
        for slot in slots:
            base = xs[slot // 2] * 2 + (c if slot % 2 == 0 else o)
            for src, dst in weight_parts(base, wb.at[0, slot]):
                pltpu.make_async_copy(src, dst, w_sem).start()

    fetch((0,))
    loaded(1, 6)
    for i in range(1, 4):
        pack(i)
    swap = remote(other, buf.at[1], peer_sem.at[0], peer_sem.at[1], peer)
    swap.start()
    fetch(range(1, 8))

    pltpu.make_async_copy(ratio, ratio, hid_sem.at[2]).wait()
    for k in range(4):
        row = pl.ds(c * 4 + k, 1)
        value = ratio[0, row, :].astype(jnp.float32) / ratio[1, row, :].astype(jnp.float32)
        beta[pl.ds(k * QUARTER, QUARTER), :] = jnp.broadcast_to(value, (QUARTER, 128)).T
    for h in range(2):
        for slot in range(8):
            wb[h, slot, pl.ds(FEATS, 128), :] = jnp.zeros((128, HALF), jnp.bfloat16)

    seen = set()

    def weights(slot):
        if not seen:
            own = wb.at[0, :, pl.ds(0, WIRE)]
            pltpu.make_async_copy(own, own, w_sem).wait()
        group = GROUP[slot]
        if group in seen:
            return
        seen.add(group)
        got = wb.at[1, pl.ds(GROUP.index(group), GROUP.count(group)), pl.ds(0, WIRE)]
        remote(got, got, ws_sem, wr_sem.at[group], peer).wait_recv()

    def multiply(slot, offsets, first=False):
        weights(slot)
        parts = [buf[slot, block(i), :] for i in offsets]
        left = parts[0] if len(parts) == 1 else jnp.concatenate(parts, axis=0)
        for h in range(2):
            policy = jnp.dot(left[:, :512], wb[h, slot, pl.ds(0, 512), :], preferred_element_type=jnp.float32)
            ref = jnp.dot(left[:, 384:], wb[h, slot, pl.ds(512, 512), :], preferred_element_type=jnp.float32)
            for n, i in enumerate(offsets):
                b = jnp.concatenate([beta[block(i), :]] * 4, axis=1)
                at = slice(n * QUARTER, (n + 1) * QUARTER)
                value = (1.0 - b) * policy[at] + b * ref[at]
                acc[h, block(i), :] = value if first else acc[h, block(i), :] + value

    def swap_rows(offset):
        return remote(
            acc.at[1, block(offset)], theirs.at[block(offset)], far_sem.at[0], far_sem.at[1], peer
        )

    def finish(offset):
        tiles = [acc[h, block(offset), pl.ds(j * 128, 128)] for h in range(2) for j in range(4)]
        high = functools.reduce(jnp.maximum, tiles)
        total = functools.reduce(jnp.add, [jnp.exp(t - high) for t in tiles])
        high, total = high.T, total.T
        top = jnp.max(high, axis=0, keepdims=True)
        summed = jnp.sum(total * jnp.exp(high - top), axis=0, keepdims=True)
        quarter = (colour + offset) % 4
        stat[pl.ds(quarter, 1), :] = top
        stat[pl.ds(quarter + 4, 1), :] = summed
        swap_rows(offset).start()

    def spread(r):
        if r >= 3 * PIECES:
            k = r - 3 * PIECES
            for flow in (YP, ZP):
                slot, _, _ = place(flow, r)
                send(flow, r, (buf.at[slot], rows(1, k)))
        plus, minus = arrived(XP, r), arrived(XM, r)
        if r < 3 * PIECES:
            for flow in (YP, YM):
                send(flow, r, plus)
            for flow in (ZP, ZM):
                send(flow, r, minus)
        if r < 2 * PIECES:
            if r % 2 == 0:
                send(XP, 2 * PIECES + r // 2, plus)
            else:
                send(XM, 2 * PIECES + r // 2, minus)
        if 2 * PIECES <= r < 3 * PIECES:
            k = r - 2 * PIECES
            send(XP, 3 * PIECES + k, (buf.at[0], rows(2, k)))
            send(XM, 3 * PIECES + k, (other, rows(2, k)), cross=True)

    def relay(r):
        got = {flow: arrived(flow, r) for flow in (YP, YM, ZP, ZM)}
        if 2 * PIECES <= r < 3 * PIECES:
            send(YM, PIECES + r, got[YM])
            send(ZM, PIECES + r, got[ZM])

    tasks = {
        0: [lambda: multiply(0, (0, 1, 2, 3), first=True)],
        3: [lambda: (swap.wait_recv(), multiply(1, (0, 1, 2, 3)))],
        7: [lambda: multiply(2, (0,)), lambda: multiply(3, (0,))],
        8: [lambda: multiply(4, (0,)), lambda: multiply(5, (0,))],
        10: [lambda: multiply(2, (1, 3))],
        11: [lambda: multiply(3, (1, 3)), lambda: multiply(4, (1, 3))],
        12: [lambda: multiply(5, (1, 3)), lambda: multiply(6, (0,))],
        13: [lambda: multiply(7, (0,))],
        14: [lambda: multiply(6, (1, 3)), lambda: finish(0)],
        15: [lambda: multiply(7, (1, 3)), lambda: multiply(2, (2,))],
        16: [lambda: multiply(5, (2,)), lambda: finish(1)],
        17: [lambda: finish(3)],
    }
    tasks[18] = [functools.partial(multiply, s, (2,)) for s in (3, 4, 6, 7)] + [lambda: finish(2)]
    for r in range(4 * PIECES + LAG):
        if r < 4 * PIECES:
            spread(r)
        if r >= LAG:
            relay(r - LAG)
        for task in tasks.get(r, ()):
            task()

    def combine(pairs):
        top = functools.reduce(jnp.maximum, [p[0] for p in pairs])
        return top, functools.reduce(jnp.add, [p[1] * jnp.exp(p[0] - top) for p in pairs])

    def halves(ref):
        return ref[pl.ds(0, 4), :], ref[pl.ds(4, 4), :]

    for k in range(1, 16):
        device = (z, (y + k // 4) % 4, (x + k % 4) % 4, c)
        remote(stat, xyin.at[k], xy_sem.at[0], xy_sem.at[1], device).start()
    plane = xyin.at[pl.ds(1, 15)]
    plane = remote(plane, plane, xy_sem.at[0], xy_sem.at[1], peer)
    plane.wait_recv()
    top, total = combine([halves(stat)] + [halves(xyin.at[k]) for k in range(1, 16)])
    stat2[pl.ds(0, 4), :] = top
    stat2[pl.ds(4, 4), :] = total
    for k in range(1, 16):
        device = ((z + k % 8) % 8, y, x, c if k < 8 else o)
        remote(stat2, zin.at[k], z_sem.at[0], z_sem.at[1], device).start()
    line = zin.at[pl.ds(1, 15)]
    line = remote(line, line, z_sem.at[0], z_sem.at[1], peer)
    line.wait_recv()
    top, total = combine([(top, total)] + [halves(zin.at[k]) for k in range(1, 8)])
    value = top + jnp.log(total)
    top, total = combine([halves(zin.at[k]) for k in range(8, 16)])
    other_value = top + jnp.log(total)
    swapped = remote(theirs, theirs, far_sem.at[0], far_sem.at[1], peer)
    swapped.wait_recv()
    for i in range(4):
        at = pl.ds(i * QUARTER, QUARTER)
        for core, source, log in ((c, acc.at[0], value), (o, theirs, other_value)):
            column = jnp.broadcast_to(log[i : i + 1, :], (QUARTER, 128)).T
            here = pl.ds(pl.multiple_of(core * HALF + i * QUARTER, QUARTER), QUARTER)
            out[here, :] = source[at, :] - jnp.concatenate([column] * 4, axis=1)

    plane.wait_send()
    line.wait_send()
    for flow in range(6):
        remote(buf.at[0], buf.at[0], send_sem.at[flow], recv_sem.at[flow, 0], peer).wait_send()
    gone = wb.at[0, :, pl.ds(0, WIRE)]
    remote(gone, gone, ws_sem, wr_sem.at[0], peer).wait_send()
    swap.wait_send()
    swapped.wait_send()


def body(policy_hidden, ref_hidden, mix_num, mix_den, policy_unembed, ref_unembed):
    hbm = pl.BlockSpec(memory_space=pltpu.HBM)
    vmem = pl.BlockSpec(memory_space=pltpu.VMEM)
    stay = functools.partial(pltpu.with_memory_space_constraint, memory_space=pltpu.HBM)
    dma = pltpu.SemaphoreType.DMA
    return pl.pallas_call(
        kernel,
        out_shape=pltpu.VMEM((2 * HALF, HALF), jnp.float32),
        in_specs=[hbm] * 6,
        out_specs=vmem,
        scratch_shapes=[
            pltpu.VMEM((8, HALF, WIRE), jnp.bfloat16),
            pltpu.VMEM((HALF, WIRE), jnp.bfloat16),
            pltpu.VMEM((2, FEATS, 2 * HALF), jnp.bfloat16),
            pltpu.VMEM((2, 8, 1024, HALF), jnp.bfloat16),
            pltpu.VMEM((2, HALF, HALF), jnp.float32),
            pltpu.VMEM((HALF, HALF), jnp.float32),
            pltpu.VMEM((2, 8, 128), jnp.int32),
            pltpu.VMEM((HALF, 128), jnp.float32),
            pltpu.VMEM((8, 128), jnp.float32),
            pltpu.VMEM((16, 8, 128), jnp.float32),
            pltpu.VMEM((8, 128), jnp.float32),
            pltpu.VMEM((16, 8, 128), jnp.float32),
            dma((3,)),
            dma(()),
            dma((5,)),
            dma(()),
            dma((6, 4 * PIECES)),
            dma((6,)),
            dma((2,)),
            dma((2,)),
            dma((2,)),
            dma((2,)),
        ],
        compiler_params=pltpu.CompilerParams(collective_id=0, has_side_effects=True, vmem_limit_bytes=44 * 2**20),
        name="mixture",
    )(
        stay(policy_hidden.T),
        stay(ref_hidden.T),
        stay(mix_num.reshape(8, 128)),
        stay(mix_den.reshape(8, 128)),
        stay(policy_unembed),
        stay(ref_unembed),
    )


def solution(mesh):
    finer = Mesh(mesh.devices.reshape(8, 4, 4, 2), VROW_VCOL)
    placed = (P(None, VCOL), P(None, VCOL), P(), P(), P(None, VROW_VCOL), P(None, VROW_VCOL))
    return jax.shard_map(
        body, mesh=finer, in_specs=placed, out_specs=P(None, VROW_VCOL), check_vma=False
    )
```

time: 62.9 us -> 50.3 us (0.80)
  Pallas kernels: 55.3 us -> 48.9 us
  other arithmetic: 3.11 us -> 0 us
  local copies, waits for them, and re-layouts: 4.33 us -> 1.32 us
    pallas_call x1, Pallas kernels: 55.3 us -> 48.9 us  [body(): pl.pallas_call(kernel, out_shape=pltpu.VMEM((2 * HALF, HALF), jnp.float32...]
    sub x1 -> x0, other arithmetic: 3.11 us -> none  [body(): return mixed - lse[:, :4].reshape(2 * HALF, 1)]
    unnamed x4 -> x1, local copies, waits for them, and re-layouts: 3.63 us -> 1.32 us
    slice x1 -> x0, local copies, waits for them, and re-layouts: 0.7 us -> none  [body(): return mixed - lse[:, :4].reshape(2 * HALF, 1)]
where the time goes in v2:
time: 50.3 us; the launch traced here: 50.2 us
  Pallas kernels  48.9 us (97%)
  local copies, waits for them, and re-layouts  1.32 us (3%)
    pallas_call x1, Pallas kernels, body(): pl.pallas_call(kernel, out_shape=pltpu.VMEM((2 * HALF, HALF), jnp.float32...  48.9 us
    unnamed x1, local copies, waits for them, and re-layouts  1.32 us

profile of v2, /device:TPU:1, one launch (start us, length us, event | category | flops | bytes accessed | tf_op | source)
XLA Modules:
  0.0 50.2 jit_solution(9559861877783429724)
XLA Ops:
  0.0 48.9 %mixture.1 = f32[1024,512]{1,0:T(8,128)S(1)} custom-call(bf16[448,1024]{1,0:T(8,128)(2,1)} %bitcast.4, bf16[448,1024]{1,0:T(8,128)(2,1)} %bitcast.5, s32[8,128]{1,0:T(8,128)} %bitcast.6, s32[8,128]{1,0:T(8,128)} %bitcast.7, bf16[3584,512]{1,0:T(8,128)(2,1)} %pw.1, bf16[3584,512]{1,0:T(8,128)(2,1)} %rw.1), custom_call_target="tpu_custom_call" | custom-call | tf_op jit(solution)/shard_map/mixture/pallas_call | solution.py:311
  48.9 1.3 %copy.8 = f32[1024,512]{1,0:T(8,128)} copy(f32[1024,512]{1,0:T(8,128)S(1)} %mixture.1) | data formatting | bytes 4194304
